TPU v7x, 32 devices: a whole 2x2x4 slice. The times are simulated.
32 devices in a mesh: dp: 8 (over z, x), mp: 4 (over y, core).
Axes of the slice: x: 2, y: 2, z: 4, core: 2. Of those that a mesh axis runs over, the one named last changes fastest.
Arguments:
- gating_logits: bfloat16 [8, 3, 64, 7168], P('dp', None, None, 'mp'), may hold values from -6 to 6
- lifted_hidden_values: bfloat16 [8, 3, 64, 7168], P('dp', None, None, 'mp'), may hold values from -6 to 6
- loss_output_grad: bfloat16 [8, 3, 64, 2048], P('dp', None, None, 'mp'), may hold values from -160 to 160
- arrival_flags: int32 [8], P('dp'), may hold values from 0 to 1, as said below
- block_owner_map: int32 [8, 3], P('dp'), may hold values from 0 to 7, as said below
- decoder_multipliers: int32 [8, 3], P('dp'), may hold values from 1 to 4
- block_piece_number: int32 [8], replicated, may hold values from 1 to 2, as said below
Outputs:
- down_grad: float32 [2048, 7168], P('dp', 'mp')
Inputs may be any that keep to these rules, and one draw needn't show every extreme that they name: `arrival_flags`: at least one replica survives. `block_owner_map`: row i lists the partitions (i + r + k) mod 8 for k < 3, with one r for all rows. `block_piece_number`: some partition has exactly 2 live tiles.
All inputs are finite; a program needn't handle non-finite values.
Results may differ from a plain program's by a relative error of at most 0.0042.
Values may be sent and summed in bfloat16 or wider, within the bound.
A program may use at most 128 MiB of HBM per device.

v0:
```python
import functools

import jax
import jax.numpy as jnp
from jax import lax
from jax.experimental import pallas as pl
from jax.experimental.pallas import tpu as pltpu
from jax.sharding import PartitionSpec as P

TILE = 32
CHUNK = 256


def kernel(
    sizes,
    flags_ref,
    owner_ref,
    mult_ref,
    pieces_ref,
    gate_hbm,
    lift_hbm,
    cot_hbm,
    out_ref,
    gate_in,
    lift_in,
    cot_ref,
    quarters,
    hid,
    cot_all,
    cot_t,
    part,
    arrived,
    tok_mine,
    tok_g,
    tok_sum,
    tok_r,
    load_c,
    load_g,
    load_l,
    send_1,
    recv_1,
    send_2,
    recv_2,
    send_3,
    recv_3,
    send_up,
    send_dn,
    recv_h,
    send_p,
    recv_p,
    send_tg,
    recv_tg,
    send_tr,
    recv_tr,
):
    G, R, M, slots, toks, chunks, rows = sizes
    d = lax.axis_index("dp")
    m = lax.axis_index("mp")
    g = d // R
    r = d % R
    quarter = slots * toks // M

    def dev(g_to, r_to, m_to):
        return {"dp": g_to * R + r_to, "mp": m_to}

    def remote(src, dst, s, q, where):
        return pltpu.make_async_remote_copy(
            src_ref=src,
            dst_ref=dst,
            send_sem=s,
            recv_sem=q,
            device_id=where,
            device_id_type=pl.DeviceIdType.MESH,
        )

    def spread_copy(off):
        m_to = (m + off) % M
        return remote(
            cot_ref.at[pl.ds(pl.multiple_of(m_to * quarter, quarter), quarter)],
            quarters.at[m],
            send_1.at[off],
            recv_1.at[m],
            dev(g, r, m_to),
        )

    def spread_in(off):
        m_from = (m + off) % M
        return remote(
            quarters.at[m_from],
            quarters.at[m_from],
            send_1.at[off],
            recv_1.at[m_from],
            dev(g, r, m_from),
        )

    def cross_copy(off):
        g_to = (g + off) % G
        return remote(
            quarters.at[g_to], cot_all.at[m, g], send_2.at[off], recv_2.at[g], dev(g_to, r, m)
        )

    def cross_in(off):
        g_from = (g + off) % G
        return remote(
            quarters.at[g],
            cot_all.at[m, g_from],
            send_2.at[off],
            recv_2.at[g_from],
            dev(g_from, r, m),
        )

    def share_copy(off):
        return remote(
            cot_all.at[m], cot_all.at[m], send_3.at[off], recv_3.at[m], dev(g, r, (m + off) % M)
        )

    def share_in(off):
        m_from = (m + off) % M
        return remote(
            cot_all.at[m_from],
            cot_all.at[m_from],
            send_3.at[off],
            recv_3.at[m_from],
            dev(g, r, m_from),
        )

    def load(src, dst, c, sem):
        return pltpu.make_async_copy(
            src.at[:, pl.ds(c * CHUNK, CHUNK)], dst.at[c], sem.at[c]
        )

    def hop(c, origin, to, sems):
        return remote(
            hid.at[c, origin],
            hid.at[c, origin],
            sems.at[c, origin],
            recv_h.at[c, origin],
            dev(to, r, m),
        )

    up, down = (g + 1) % G, (g + G - 1) % G

    def pass_on(c, origin, has_next, to, sems):
        hop(c, origin, to, sems).wait_recv()

        @pl.when(has_next)
        def _():
            hop(c, origin, to, sems).start()

    def part_copy(c, off):
        r_to = (r + off) % R
        return remote(
            part.at[c, r_to], arrived.at[c, r], send_p.at[c, off], recv_p.at[c, r], dev(g, r_to, m)
        )

    def part_in(c, off):
        r_from = (r + off) % R
        return remote(
            part.at[c, r_from],
            arrived.at[c, r_from],
            send_p.at[c, off],
            recv_p.at[c, r_from],
            dev(g, r_from, m),
        )

    def tok_copy(off):
        return remote(
            tok_mine, tok_g.at[g], send_tg.at[off], recv_tg.at[g], dev((g + off) % G, r, m)
        )

    def tok_in(off):
        g_from = (g + off) % G
        return remote(
            tok_mine, tok_g.at[g_from], send_tg.at[off], recv_tg.at[g_from], dev(g_from, r, m)
        )

    def sum_copy(off):
        return remote(
            tok_sum, tok_r.at[r], send_tr.at[off], recv_tr.at[r], dev(g, (r + off) % R, m)
        )

    def sum_in(off):
        r_from = (r + off) % R
        return remote(
            tok_sum, tok_r.at[r_from], send_tr.at[off], recv_tr.at[r_from], dev(g, r_from, m)
        )

    def over_r(body):
        def step(off, carry):
            body(off)
            return carry

        lax.fori_loop(1, R, step, 0)

    load_cot = pltpu.make_async_copy(cot_hbm, cot_ref, load_c)
    load_cot.start()
    for c in range(chunks):
        load(gate_hbm, gate_in, c, load_g).start()
        load(lift_hbm, lift_in, c, load_l).start()

    barrier = pltpu.get_barrier_semaphore()

    def greet(where):
        pl.semaphore_signal(
            barrier, inc=1, device_id=where, device_id_type=pl.DeviceIdType.MESH
        )

    for off in range(1, M):
        greet(dev(g, r, (m + off) % M))
    for off in range(1, G):
        greet(dev((g + off) % G, r, m))
    over_r(lambda off: greet(dev(g, (r + off) % R, m)))
    load_cot.wait()
    quarters[m] = cot_ref[pl.ds(pl.multiple_of(m * quarter, quarter), quarter), :]
    pl.semaphore_wait(barrier, M - 1 + G - 1 + R - 1)

    for off in range(1, M):
        spread_copy(off).start()

    flag = flags_ref[0].astype(jnp.float32)
    scales = []
    token_sum = jnp.float32(0)
    row = lax.broadcasted_iota(jnp.int32, (toks, CHUNK), 0)
    for k in range(slots):
        live = pieces_ref[owner_ref[0, k]] * TILE
        weight = flag * mult_ref[0, k].astype(jnp.float32)
        scales.append(jnp.where(row < live, weight, 0.0))
        token_sum = token_sum + weight * live.astype(jnp.float32)

    for c in range(chunks):
        load(gate_hbm, gate_in, c, load_g).wait()
        load(lift_hbm, lift_in, c, load_l).wait()
        for k in range(slots):
            rk = pl.ds(k * toks, toks)
            v = gate_in[c, rk, :].astype(jnp.float32)
            u = lift_in[c, rk, :].astype(jnp.float32)
            h = v / (1.0 + jnp.exp(-v)) * u * scales[k]
            hid[c, g, rk, :] = h.astype(jnp.bfloat16)
        if c == 0:
            tok_mine[...] = jnp.full(tok_mine.shape, token_sum, jnp.float32)

        @pl.when(g < G - 1)
        def _():
            hop(c, g, up, send_up).start()

        @pl.when(g > 0)
        def _():
            hop(c, g, down, send_dn).start()

        if c == 0:
            for off in range(1, G):
                tok_copy(off).start()
            for off in range(1, M):
                spread_in(off).wait_recv()
            cot_all[m, g] = quarters[g]
            for off in range(1, G):
                cross_copy(off).start()

    for off in range(1, G):
        cross_in(off).wait_recv()
    for off in range(1, M):
        share_copy(off).start()
    for off in range(1, M):
        share_in(off).wait_recv()

    for i in range(G):
        n = slots * toks
        block = jnp.concatenate([cot_all[j, i] for j in range(M)], axis=0)
        cot_t[:, pl.ds(i * n, n)] = block.T

    for c in range(chunks):
        for k in range(1, G):

            @pl.when(g >= k)
            def _():
                pass_on(c, (g + G - k) % G, g < G - 1, up, send_up)

            @pl.when(g + k < G)
            def _():
                pass_on(c, (g + k) % G, g > 0, down, send_dn)

        block = hid[c].reshape(G * slots * toks, CHUNK)
        if c == 0:
            total = tok_mine[...]
            for off in range(1, G):
                tok_in(off).wait_recv()
                total = total + tok_g[(g + off) % G]
            tok_sum[...] = total

        def other(off):
            r_to = (r + off) % R
            left = cot_t[pl.ds(pl.multiple_of(r_to * rows, rows), rows), :]
            prod = jnp.dot(left, block, preferred_element_type=jnp.float32)
            part[c, r_to] = prod.astype(jnp.bfloat16)
            part_copy(c, off).start()

        over_r(other)
        if c == 0:
            over_r(lambda off: sum_copy(off).start())
        left = cot_t[pl.ds(pl.multiple_of(r * rows, rows), rows), :]
        out_ref[:, pl.ds(c * CHUNK, CHUNK)] = jnp.dot(
            left, block, preferred_element_type=jnp.float32
        )

    def add_tokens(off, total):
        sum_in(off).wait_recv()
        return total + tok_r[(r + off) % R]

    total = lax.fori_loop(1, R, add_tokens, tok_sum[...])
    inverse = (1.0 / total)[0:1, 0:1]
    for c in range(chunks):
        cols = pl.ds(c * CHUNK, CHUNK)

        def add_part(off):
            part_in(c, off).wait_recv()
            out_ref[:, cols] = out_ref[:, cols] + arrived[c, (r + off) % R].astype(jnp.float32)

        over_r(add_part)
        out_ref[:, cols] = out_ref[:, cols] * inverse

    for off in range(1, M):
        spread_copy(off).wait_send()
        share_copy(off).wait_send()

    for off in range(1, G):
        tok_copy(off).wait_send()
        cross_copy(off).wait_send()

    for c in range(chunks):
        for i in range(G):

            @pl.when(jnp.logical_and(i <= g, g < G - 1))
            def _():
                hop(c, i, up, send_up).wait_send()

            @pl.when(jnp.logical_and(i >= g, g > 0))
            def _():
                hop(c, i, down, send_dn).wait_send()

    def drain(off):
        sum_copy(off).wait_send()
        for c in range(chunks):
            part_copy(c, off).wait_send()

    over_r(drain)


def on_device(
    mesh_shape,
    gating_logits,
    lifted_hidden_values,
    loss_output_grad,
    arrival_flags,
    block_owner_map,
    decoder_multipliers,
    block_piece_number,
):
    dp, M = mesh_shape
    G = M
    R = dp // G
    _, slots, toks, width = gating_logits.shape
    feats = loss_output_grad.shape[3]
    rows = feats * M // dp
    chunks = width // CHUNK
    n = slots * toks
    sizes = (G, R, M, slots, toks, chunks, rows)
    smem = pl.BlockSpec(memory_space=pltpu.SMEM)
    vmem = pl.BlockSpec(memory_space=pltpu.VMEM)
    dma = pltpu.SemaphoreType.DMA
    bf, f32 = jnp.bfloat16, jnp.float32
    return pl.pallas_call(
        functools.partial(kernel, sizes),
        out_shape=jax.ShapeDtypeStruct((rows, width), f32),
        in_specs=[smem] * 4 + [pl.BlockSpec(memory_space=pl.ANY)] * 3,
        out_specs=vmem,
        scratch_shapes=[
            pltpu.VMEM((chunks, n, CHUNK), bf),
            pltpu.VMEM((chunks, n, CHUNK), bf),
            pltpu.VMEM((n, feats), bf),
            pltpu.VMEM((M, n // M, feats), bf),
            pltpu.VMEM((chunks, G, n, CHUNK), bf),
            pltpu.VMEM((M, G, n // M, feats), bf),
            pltpu.VMEM((feats, G * n), bf),
            pltpu.VMEM((chunks, R, rows, CHUNK), bf),
            pltpu.VMEM((chunks, R, rows, CHUNK), bf),
            pltpu.VMEM((8, 128), f32),
            pltpu.VMEM((G, 8, 128), f32),
            pltpu.VMEM((8, 128), f32),
            pltpu.VMEM((R, 8, 128), f32),
            dma,
            dma((chunks,)),
            dma((chunks,)),
            dma((M,)),
            dma((M,)),
            dma((G,)),
            dma((G,)),
            dma((M,)),
            dma((M,)),
            dma((chunks, G)),
            dma((chunks, G)),
            dma((chunks, G)),
            dma((chunks, R)),
            dma((chunks, R)),
            dma((G,)),
            dma((G,)),
            dma((R,)),
            dma((R,)),
        ],
        compiler_params=pltpu.CompilerParams(
            collective_id=0, has_side_effects=True
        ),
    )(
        arrival_flags,
        block_owner_map,
        decoder_multipliers,
        block_piece_number,
        gating_logits.reshape(n, width),
        lifted_hidden_values.reshape(n, width),
        loss_output_grad.reshape(n, feats),
    )


def solution(mesh):
    shape = (mesh.shape["dp"], mesh.shape["mp"])
    return jax.shard_map(
        functools.partial(on_device, shape),
        mesh=mesh,
        in_specs=(
            P("dp", None, None, "mp"),
            P("dp", None, None, "mp"),
            P("dp", None, None, "mp"),
            P("dp"),
            P("dp", None),
            P("dp", None),
            P(),
        ),
        out_specs=P("dp", "mp"),
        check_vma=False,
    )
```

profile of v0, /device:TPU:0, one launch (start us, length us, event | category | flops | bytes accessed | tf_op | source)
XLA Modules:
  0.0 71.1 jit_solution(9299322002407830843)
XLA Ops:
  0.7 67.6 %shard_map.73 = f32[256,1792]{1,0:T(8,128)} custom-call(s32[1]{0:T(128)S(6)} %copy.9.flags_ref, s32[1,3]{1,0:T(1,128)} %owner_ref.1, s32[1,3]{1,0:T(1,128)} %mult_ref.1, s32[8]{0:T(128)} %pieces_ref.1, bf16[192,1792]{1,0:T(8,128)(2,1)} %bitcast.3, bf16[192,1792]{1,0:T(8,128)(2,1)} %bitcast.4, bf16[192,512]{1,0:T(8,128)(2,1)} %bitcast.5), custom_call_target="tpu_custom_call" | custom-call | tf_op jit(solution)/shard_map/pallas_call | solution.py:371
  68.2 2.8 %copy.10 = f32[256,1792]{1,0:T(8,128)} copy(f32[256,1792]{1,0:T(8,128)} %shard_map.73) | data formatting | bytes 3670016
where the time goes:
time: 71.2 us; the launch traced here: 71.1 us
  Pallas kernels  67.6 us (95%)
  local copies, waits for them, and re-layouts  2.85 us (4%)
    pallas_call x1, Pallas kernels, on_device(): pl.pallas_call(functools.partial(kernel, sizes), out_shape=jax.ShapeDtype...  67.6 us
    unnamed x1, local copies, waits for them, and re-layouts  2.85 us

commit v1 on v0

--- a/solution.py
+++ b/solution.py
@@ -9,6 +9,11 @@
 
 TILE = 32
 CHUNK = 256
+SHARED = (3, 5)
+AHEAD = 3
+EARLY = 2
+STAGES = (1, 2, 2)
+LAG = 2
 
 
 def kernel(
@@ -34,6 +39,14 @@
     tok_g,
     tok_sum,
     tok_r,
+    cot_x,
+    cot_own,
+    cot_e,
+    mine_e,
+    give_e,
+    take_e,
+    sum_e,
+    from_e,
     load_c,
     load_g,
     load_l,
@@ -52,13 +65,33 @@
     recv_tg,
     send_tr,
     recv_tr,
+    send_x,
+    recv_x,
+    send_y,
+    recv_y,
+    send_e,
+    recv_e,
+    send_f,
+    recv_f,
+    send_r,
 ):
-    G, R, M, slots, toks, chunks, rows = sizes
+    G, R, M, slots, toks, chunks, rows, shared = sizes
+    n = slots * toks
     d = lax.axis_index("dp")
     m = lax.axis_index("mp")
     g = d // R
     r = d % R
-    quarter = slots * toks // M
+    quarter = n // M
+    pair = M == 4
+    m1 = m + 1 - 2 * (m % 2)
+    m2 = m + 2 - 4 * (m // 2)
+    m3 = m1 + 2 - 4 * (m1 // 2)
+
+    at_edge = jnp.logical_or(g == 0, g == G - 1)
+    is_dn = g == 1
+    helper = jnp.logical_or(g == 1, g == G - 2)
+    base = jnp.where(is_dn, 1, 0)
+    edge = jnp.where(is_dn, 0, G - 1)
 
     def dev(g_to, r_to, m_to):
         return {"dp": g_to * R + r_to, "mp": m_to}
@@ -93,36 +126,81 @@
             dev(g, r, m_from),
         )
 
-    def cross_copy(off):
-        g_to = (g + off) % G
-        return remote(
-            quarters.at[g_to], cot_all.at[m, g], send_2.at[off], recv_2.at[g], dev(g_to, r, m)
-        )
-
-    def cross_in(off):
-        g_from = (g + off) % G
+    def cross_copy(g_to):
+        return remote(
+            quarters.at[g_to], cot_all.at[m, g], send_2.at[g_to], recv_2.at[g], dev(g_to, r, m)
+        )
+
+    def cross_in(g_from):
         return remote(
             quarters.at[g],
             cot_all.at[m, g_from],
-            send_2.at[off],
+            send_2.at[g_from],
             recv_2.at[g_from],
             dev(g_from, r, m),
         )
 
-    def share_copy(off):
-        return remote(
-            cot_all.at[m], cot_all.at[m], send_3.at[off], recv_3.at[m], dev(g, r, (m + off) % M)
-        )
-
-    def share_in(off):
-        m_from = (m + off) % M
-        return remote(
-            cot_all.at[m_from],
-            cot_all.at[m_from],
-            send_3.at[off],
-            recv_3.at[m_from],
-            dev(g, r, m_from),
-        )
+    def extra_copy(g_to, block, s):
+        return remote(
+            quarters.at[block], cot_x.at[m, g], send_x.at[s], recv_x.at[g], dev(g_to, r, m)
+        )
+
+    def extra_relay(g_from):
+        return remote(
+            cot_x.at[m, g_from],
+            cot_all.at[m, g_from],
+            send_r.at[g_from],
+            recv_2.at[g_from],
+            dev(edge, r, m),
+        )
+
+    def extra_in(g_from):
+        return remote(
+            quarters.at[0], cot_x.at[m, g_from], send_x.at[0], recv_x.at[g_from], dev(g_from, r, m)
+        )
+
+    def share(src, buf, origin, i, way, to, sends, recvs):
+        return remote(
+            src, buf.at[origin, i], sends.at[way, i], recvs.at[origin, i], dev(g, r, to)
+        )
+
+    peers = [m1, m2] if pair else [(m + off) % M for off in range(1, M)]
+
+    def share_out(buf, src, i, sends, recvs):
+        for way, to in enumerate(peers):
+            share(src, buf, m, i, way, to, sends, recvs).start()
+
+    def relay(buf, i, sends, recvs):
+        if pair:
+            share(buf.at[m2, i], buf, m2, i, 2, m1, sends, recvs).wait_recv()
+            share(buf.at[m2, i], buf, m2, i, 2, m1, sends, recvs).start()
+
+    def share_end(buf, i, sends, recvs):
+        for o in [m1, m3] if pair else peers:
+            share(buf.at[o, i], buf, o, i, 0, m1, sends, recvs).wait_recv()
+
+    def share_drain(buf, i, sends, recvs):
+        for way, to in enumerate(peers):
+            share(buf.at[m, i], buf, m, i, way, to, sends, recvs).wait_send()
+        if pair:
+            share(buf.at[m2, i], buf, m2, i, 2, m1, sends, recvs).wait_send()
+
+    def others(body):
+        for k in range(1, G):
+
+            @pl.when(g >= k)
+            def _():
+                body(g - k)
+
+            @pl.when(g + k < G)
+            def _():
+                body(g + k)
+
+    def extras(body):
+        @pl.when(helper)
+        def _():
+            for k in range(1, G - 1):
+                body(jnp.where(is_dn, g + k, g - k))
 
     def load(src, dst, c, sem):
         return pltpu.make_async_copy(
@@ -140,12 +218,33 @@
 
     up, down = (g + 1) % G, (g + G - 1) % G
 
+    def goes_up(c):
+        return g < (G - 2 if c in shared else G - 1)
+
+    def goes_down(c):
+        return g > (1 if c in shared else 0)
+
     def pass_on(c, origin, has_next, to, sems):
         hop(c, origin, to, sems).wait_recv()
 
         @pl.when(has_next)
         def _():
             hop(c, origin, to, sems).start()
+
+    def receive(c, k):
+        from_left = g >= k
+        from_right = g + k < G
+        if c in shared:
+            from_left = jnp.logical_and(from_left, g < G - 1)
+            from_right = jnp.logical_and(from_right, g > 0)
+
+        @pl.when(from_left)
+        def _():
+            pass_on(c, (g + G - k) % G, goes_up(c), up, send_up)
+
+        @pl.when(from_right)
+        def _():
+            pass_on(c, (g + k) % G, goes_down(c), down, send_dn)
 
     def part_copy(c, off):
         r_to = (r + off) % R
@@ -163,6 +262,14 @@
             dev(g, r_from, m),
         )
 
+    def swap_e(b):
+        return remote(
+            give_e.at[b], take_e.at[b], send_e.at[b], recv_e.at[b], dev(g, (r + 1) % R, m)
+        )
+
+    def final_e(b, to):
+        return remote(sum_e.at[b], from_e.at[b], send_f.at[b], recv_f.at[b], dev(to, r, m))
+
     def tok_copy(off):
         return remote(
             tok_mine, tok_g.at[g], send_tg.at[off], recv_tg.at[g], dev((g + off) % G, r, m)
@@ -210,12 +317,6 @@
     for off in range(1, G):
         greet(dev((g + off) % G, r, m))
     over_r(lambda off: greet(dev(g, (r + off) % R, m)))
-    load_cot.wait()
-    quarters[m] = cot_ref[pl.ds(pl.multiple_of(m * quarter, quarter), quarter), :]
-    pl.semaphore_wait(barrier, M - 1 + G - 1 + R - 1)
-
-    for off in range(1, M):
-        spread_copy(off).start()
 
     flag = flags_ref[0].astype(jnp.float32)
     scales = []
@@ -226,8 +327,9 @@
         weight = flag * mult_ref[0, k].astype(jnp.float32)
         scales.append(jnp.where(row < live, weight, 0.0))
         token_sum = token_sum + weight * live.astype(jnp.float32)
-
-    for c in range(chunks):
+    tok_mine[...] = jnp.full(tok_mine.shape, token_sum, jnp.float32)
+
+    def make_hidden(c):
         load(gate_hbm, gate_in, c, load_g).wait()
         load(lift_hbm, lift_in, c, load_l).wait()
         for k in range(slots):
@@ -236,104 +338,268 @@
             u = lift_in[c, rk, :].astype(jnp.float32)
             h = v / (1.0 + jnp.exp(-v)) * u * scales[k]
             hid[c, g, rk, :] = h.astype(jnp.bfloat16)
-        if c == 0:
-            tok_mine[...] = jnp.full(tok_mine.shape, token_sum, jnp.float32)
-
-        @pl.when(g < G - 1)
+
+    def send_hidden(c):
+        @pl.when(goes_up(c))
         def _():
             hop(c, g, up, send_up).start()
 
-        @pl.when(g > 0)
+        @pl.when(goes_down(c))
         def _():
             hop(c, g, down, send_dn).start()
 
-        if c == 0:
-            for off in range(1, G):
-                tok_copy(off).start()
-            for off in range(1, M):
-                spread_in(off).wait_recv()
-            cot_all[m, g] = quarters[g]
-            for off in range(1, G):
-                cross_copy(off).start()
-
+    load_cot.wait()
+    quarters[m] = cot_ref[pl.ds(pl.multiple_of(m * quarter, quarter), quarter), :]
+    make_hidden(0)
+    pl.semaphore_wait(barrier, M - 1 + G - 1 + R - 1)
+
+    for off in range(1, M):
+        spread_copy(off).start()
+    send_hidden(0)
     for off in range(1, G):
-        cross_in(off).wait_recv()
+        tok_copy(off).start()
+    for c in range(1, EARLY):
+        make_hidden(c)
+        send_hidden(c)
     for off in range(1, M):
-        share_copy(off).start()
-    for off in range(1, M):
-        share_in(off).wait_recv()
-
-    for i in range(G):
-        n = slots * toks
-        block = jnp.concatenate([cot_all[j, i] for j in range(M)], axis=0)
-        cot_t[:, pl.ds(i * n, n)] = block.T
-
-    for c in range(chunks):
-        for k in range(1, G):
-
-            @pl.when(g >= k)
-            def _():
-                pass_on(c, (g + G - k) % G, g < G - 1, up, send_up)
-
-            @pl.when(g + k < G)
-            def _():
-                pass_on(c, (g + k) % G, g > 0, down, send_dn)
-
-        block = hid[c].reshape(G * slots * toks, CHUNK)
-        if c == 0:
-            total = tok_mine[...]
-            for off in range(1, G):
-                tok_in(off).wait_recv()
-                total = total + tok_g[(g + off) % G]
-            tok_sum[...] = total
-
+        spread_in(off).wait_recv()
+    def direct(i, body):
+        if not shared:
+            body(cross_copy(i))
+            return
+        by_hand = jnp.logical_or(
+            jnp.logical_and(i == G - 1, g < G - 2), jnp.logical_and(i == 0, g > 1)
+        )
+
+        @pl.when(jnp.logical_not(by_hand))
+        def _():
+            body(cross_copy(i))
+
+    others(lambda i: direct(i, lambda copy: copy.start()))
+    if shared:
+
+        @pl.when(g < G - 2)
+        def _():
+            extra_copy(G - 2, G - 1, 0).start()
+
+        @pl.when(g > 1)
+        def _():
+            extra_copy(1, 0, 1).start()
+
+    share_out(cot_all, quarters.at[g], g, send_3, recv_3)
+    cot_all[m, g] = quarters[g]
+    if shared:
+
+        @pl.when(helper)
+        def _():
+            share_out(cot_x, quarters.at[edge], g, send_y, recv_y)
+            cot_x[m, g] = quarters[edge]
+
+    for c in range(EARLY, AHEAD):
+        make_hidden(c)
+        send_hidden(c)
+
+    def share_more():
+        if shared:
+
+            def more(i):
+                extra_in(i).wait_recv()
+                extra_relay(i).start()
+                share_out(cot_x, cot_x.at[m, i], i, send_y, recv_y)
+
+            extras(more)
+
+        def one(i):
+            cross_in(i).wait_recv()
+            share_out(cot_all, cot_all.at[m, i], i, send_3, recv_3)
+
+        others(one)
+
+    def relay_all():
+        relay(cot_all, g, send_3, recv_3)
+        others(lambda i: relay(cot_all, i, send_3, recv_3))
+        if shared:
+
+            @pl.when(helper)
+            def _():
+                relay(cot_x, g, send_y, recv_y)
+
+            extras(lambda i: relay(cot_x, i, send_y, recv_y))
+
+    def turn():
+        for i in range(G):
+            share_end(cot_all, i, send_3, recv_3)
+            block = jnp.concatenate([cot_all[j, i] for j in range(M)], axis=0)
+            cot_t[:, pl.ds(i * n, n)] = block.T
+        if shared:
+
+            @pl.when(at_edge)
+            def _():
+                block = jnp.concatenate([cot_all[j, g] for j in range(M)], axis=0)
+                cot_own[...] = block.T
+
+            @pl.when(helper)
+            def _():
+                for i in range(G - 1):
+                    share_end(cot_x, base + i, send_y, recv_y)
+                    block = jnp.concatenate([cot_x[j, base + i] for j in range(M)], axis=0)
+                    cot_e[:, pl.ds(i * n, n)] = block.T
+
+    def product(left, block):
+        return jnp.dot(left, block, preferred_element_type=jnp.float32)
+
+    def strip(ref, which):
+        return ref[pl.ds(pl.multiple_of(which * rows, rows), rows), :]
+
+    def main(c, left_ref, block):
         def other(off):
             r_to = (r + off) % R
-            left = cot_t[pl.ds(pl.multiple_of(r_to * rows, rows), rows), :]
-            prod = jnp.dot(left, block, preferred_element_type=jnp.float32)
-            part[c, r_to] = prod.astype(jnp.bfloat16)
+            part[c, r_to] = product(strip(left_ref, r_to), block).astype(jnp.bfloat16)
             part_copy(c, off).start()
 
         over_r(other)
-        if c == 0:
-            over_r(lambda off: sum_copy(off).start())
-        left = cot_t[pl.ds(pl.multiple_of(r * rows, rows), rows), :]
-        out_ref[:, pl.ds(c * CHUNK, CHUNK)] = jnp.dot(
-            left, block, preferred_element_type=jnp.float32
-        )
+        out_ref[:, pl.ds(c * CHUNK, CHUNK)] = product(strip(left_ref, r), block)
+
+    def compute(c):
+        if c not in shared:
+            main(c, cot_t, hid[c].reshape(G * n, CHUNK))
+            return
+        b = shared.index(c)
+
+        @pl.when(at_edge)
+        def _():
+            main(c, cot_own, hid[c, g])
+
+        @pl.when(jnp.logical_not(at_edge))
+        def _():
+            @pl.when(helper)
+            def _():
+                block = hid[c, pl.ds(base, G - 1)].reshape((G - 1) * n, CHUNK)
+                give_e[b] = product(strip(cot_e, (r + 1) % R), block).astype(jnp.bfloat16)
+                swap_e(b).start()
+                mine_e[b] = product(strip(cot_e, r), block)
+
+            main(c, cot_t, hid[c].reshape(G * n, CHUNK))
+
+    def hand_over(c):
+        b = shared.index(c)
+
+        @pl.when(helper)
+        def _():
+            swap_e(b).wait_recv()
+            sum_e[b] = (mine_e[b] + take_e[b].astype(jnp.float32)).astype(jnp.bfloat16)
+            final_e(b, edge).start()
+
+    def tokens_g():
+        total = tok_mine[...]
+        for off in range(1, G):
+            tok_in(off).wait_recv()
+            total = total + tok_g[(g + off) % G]
+        tok_sum[...] = total
+        over_r(lambda off: sum_copy(off).start())
 
     def add_tokens(off, total):
         sum_in(off).wait_recv()
         return total + tok_r[(r + off) % R]
 
-    total = lax.fori_loop(1, R, add_tokens, tok_sum[...])
-    inverse = (1.0 / total)[0:1, 0:1]
-    for c in range(chunks):
+    inverse = []
+
+    def finish(c):
         cols = pl.ds(c * CHUNK, CHUNK)
+        if not inverse:
+            total = lax.fori_loop(1, R, add_tokens, tok_sum[...])
+            inverse.append((1.0 / total)[0:1, 0:1])
 
         def add_part(off):
             part_in(c, off).wait_recv()
             out_ref[:, cols] = out_ref[:, cols] + arrived[c, (r + off) % R].astype(jnp.float32)
 
         over_r(add_part)
-        out_ref[:, cols] = out_ref[:, cols] * inverse
+        if c in shared:
+            b = shared.index(c)
+
+            @pl.when(at_edge)
+            def _():
+                final_e(b, down).wait_recv()
+                out_ref[:, cols] = out_ref[:, cols] + from_e[b].astype(jnp.float32)
+
+        out_ref[:, cols] = out_ref[:, cols] * inverse[0]
+
+    stage = STAGES
+    done = []
+    ready = 0
+    handed = 0
+    for t in range(chunks + 1):
+        if t < chunks:
+            receive(t, 1)
+        if t + AHEAD < chunks:
+            make_hidden(t + AHEAD)
+            send_hidden(t + AHEAD)
+        if t == stage[0]:
+            share_more()
+            tokens_g()
+        if t == stage[1]:
+            relay_all()
+        if t >= 1:
+            for k in range(2, G):
+                receive(t - 1, k)
+        if t == stage[2]:
+            turn()
+        late = ready
+        while t >= stage[2] and ready < t:
+            compute(ready)
+            ready += 1
+        for c in range(handed, late):
+            if c in shared:
+                hand_over(c)
+            handed = c + 1
+        if t >= stage[2] + LAG:
+            for c in range(t - 1 - LAG):
+                if c not in done and c not in shared:
+                    finish(c)
+                    done.append(c)
+    for c in range(handed, chunks):
+        if c in shared:
+            hand_over(c)
+    for c in range(chunks):
+        if c not in done:
+            finish(c)
 
     for off in range(1, M):
         spread_copy(off).wait_send()
-        share_copy(off).wait_send()
-
     for off in range(1, G):
         tok_copy(off).wait_send()
-        cross_copy(off).wait_send()
+    others(lambda i: direct(i, lambda copy: copy.wait_send()))
+    for i in range(G):
+        share_drain(cot_all, i, send_3, recv_3)
+    if shared:
+
+        @pl.when(g < G - 2)
+        def _():
+            extra_copy(G - 2, G - 1, 0).wait_send()
+
+        @pl.when(g > 1)
+        def _():
+            extra_copy(1, 0, 1).wait_send()
+
+        @pl.when(helper)
+        def _():
+            for i in range(G - 1):
+                share_drain(cot_x, base + i, send_y, recv_y)
+            for k in range(1, G - 1):
+                extra_relay(jnp.where(is_dn, g + k, g - k)).wait_send()
+            for b in range(len(shared)):
+                swap_e(b).wait_send()
+                final_e(b, edge).wait_send()
 
     for c in range(chunks):
         for i in range(G):
 
-            @pl.when(jnp.logical_and(i <= g, g < G - 1))
+            @pl.when(jnp.logical_and(i <= g, goes_up(c)))
             def _():
                 hop(c, i, up, send_up).wait_send()
 
-            @pl.when(jnp.logical_and(i >= g, g > 0))
+            @pl.when(jnp.logical_and(i >= g, goes_down(c)))
             def _():
                 hop(c, i, down, send_dn).wait_send()
 
@@ -363,7 +629,10 @@
     rows = feats * M // dp
     chunks = width // CHUNK
     n = slots * toks
-    sizes = (G, R, M, slots, toks, chunks, rows)
+    shared = SHARED if R == 2 and G >= 4 else ()
+    sizes = (G, R, M, slots, toks, chunks, rows, shared)
+    nb = max(len(shared), 1)
+    far = G if shared else 1
     smem = pl.BlockSpec(memory_space=pltpu.SMEM)
     vmem = pl.BlockSpec(memory_space=pltpu.VMEM)
     dma = pltpu.SemaphoreType.DMA
@@ -387,6 +656,14 @@
             pltpu.VMEM((G, 8, 128), f32),
             pltpu.VMEM((8, 128), f32),
             pltpu.VMEM((R, 8, 128), f32),
+            pltpu.VMEM((M, far, n // M, feats), bf),
+            pltpu.VMEM((feats, n), bf),
+            pltpu.VMEM((feats, (G - 1) * n), bf),
+            pltpu.VMEM((nb, rows, CHUNK), f32),
+            pltpu.VMEM((nb, rows, CHUNK), bf),
+            pltpu.VMEM((nb, rows, CHUNK), bf),
+            pltpu.VMEM((nb, rows, CHUNK), bf),
+            pltpu.VMEM((nb, rows, CHUNK), bf),
             dma,
             dma((chunks,)),
             dma((chunks,)),
@@ -394,8 +671,8 @@
             dma((M,)),
             dma((G,)),
             dma((G,)),
-            dma((M,)),
-            dma((M,)),
+            dma((M, G)),
+            dma((M, G)),
             dma((chunks, G)),
             dma((chunks, G)),
             dma((chunks, G)),
@@ -405,6 +682,15 @@
             dma((G,)),
             dma((R,)),
             dma((R,)),
+            dma((2,)),
+            dma((G,)),
+            dma((M, G)),
+            dma((M, G)),
+            dma((nb,)),
+            dma((nb,)),
+            dma((nb,)),
+            dma((nb,)),
+            dma((G,)),
         ],
         compiler_params=pltpu.CompilerParams(
             collective_id=0, has_side_effects=True

time: 71.2 us -> 59.9 us (0.84)
  Pallas kernels: 67.6 us -> 56.2 us
    pallas_call x1, Pallas kernels: 67.6 us -> 56.2 us  [on_device(): pl.pallas_call(functools.partial(kernel, sizes), out_shape=jax.ShapeDtype...]
where the time goes in v1:
time: 59.9 us; the launch traced here: 59.7 us
  Pallas kernels  56.2 us (94%)
  local copies, waits for them, and re-layouts  2.85 us (5%)
  between operations  0.66 us (1%)
    pallas_call x1, Pallas kernels, on_device(): pl.pallas_call(functools.partial(kernel, sizes), out_shape=jax.ShapeDtype...  56.2 us
    unnamed x1, local copies, waits for them, and re-layouts  2.85 us

profile of v1, /device:TPU:0, one launch (start us, length us, event | category | flops | bytes accessed | tf_op | source)
XLA Modules:
  0.0 59.7 jit_solution(9323470410392497447)
XLA Ops:
  0.7 56.2 %shard_map.73 = f32[256,1792]{1,0:T(8,128)} custom-call(s32[1]{0:T(128)S(6)} %copy.9.flags_ref, s32[1,3]{1,0:T(1,128)} %owner_ref.1, s32[1,3]{1,0:T(1,128)} %mult_ref.1, s32[8]{0:T(128)} %pieces_ref.1, bf16[192,1792]{1,0:T(8,128)(2,1)} %bitcast.3, bf16[192,1792]{1,0:T(8,128)(2,1)} %bitcast.4, bf16[192,512]{1,0:T(8,128)(2,1)} %bitcast.5), custom_call_target="tpu_custom_call" | custom-call | tf_op jit(solution)/shard_map/pallas_call | solution.py:640
  56.9 2.8 %copy.10 = f32[256,1792]{1,0:T(8,128)} copy(f32[256,1792]{1,0:T(8,128)} %shard_map.73) | data formatting | bytes 3670016

commit v2 on v1

--- a/solution.py
+++ b/solution.py
@@ -9,11 +9,16 @@
 
 TILE = 32
 CHUNK = 256
-SHARED = (3, 5)
-AHEAD = 3
+SHARED = (2, 5)
+AHEAD = (2, 3, 4)
 EARLY = 2
-STAGES = (1, 2, 2)
-LAG = 2
+MID = 2
+NEXT = 3
+STAGES = (0, 0, 2, 2, 3, 5)
+EXTRA = (2, 7, 7)
+LAG = 1
+HAND = 2
+TOKENS = 5
 
 
 def kernel(
@@ -185,8 +190,11 @@
         if pair:
             share(buf.at[m2, i], buf, m2, i, 2, m1, sends, recvs).wait_send()
 
-    def others(body):
-        for k in range(1, G):
+    def others(reach, body):
+        for k in reach:
+            if k == 0:
+                body(g)
+                continue
 
             @pl.when(g >= k)
             def _():
@@ -339,30 +347,57 @@
             h = v / (1.0 + jnp.exp(-v)) * u * scales[k]
             hid[c, g, rk, :] = h.astype(jnp.bfloat16)
 
-    def send_hidden(c):
-        @pl.when(goes_up(c))
-        def _():
-            hop(c, g, up, send_up).start()
-
-        @pl.when(goes_down(c))
-        def _():
-            hop(c, g, down, send_dn).start()
+    if G >= 3:
+        up_ways = (
+            jnp.logical_and(g >= 1, g < G - 2),
+            g == G - 2,
+            g == 0,
+        )
+        down_ways = (
+            jnp.logical_and(g > 1, g <= G - 2),
+            g == 1,
+            g == G - 1,
+        )
+    else:
+        up_ways, down_ways = (g < G - 1,), (g > 0,)
+    ways = len(up_ways)
+    made = [0]
+    sent = [0] * ways
+
+    def send_to(*counts):
+        counts = [min(c, chunks) for c in counts[-ways:]]
+        for c in range(max(counts)):
+            while made[0] <= c:
+                make_hidden(made[0])
+                made[0] += 1
+            for way in range(ways):
+                if sent[way] <= c < counts[way] and not (way == 1 and c in shared):
+
+                    @pl.when(up_ways[way])
+                    def _():
+                        hop(c, g, up, send_up).start()
+
+                    @pl.when(down_ways[way])
+                    def _():
+                        hop(c, g, down, send_dn).start()
+
+        for way in range(ways):
+            sent[way] = max(sent[way], counts[way])
 
     load_cot.wait()
     quarters[m] = cot_ref[pl.ds(pl.multiple_of(m * quarter, quarter), quarter), :]
     make_hidden(0)
+    made[0] = 1
     pl.semaphore_wait(barrier, M - 1 + G - 1 + R - 1)
 
     for off in range(1, M):
         spread_copy(off).start()
-    send_hidden(0)
     for off in range(1, G):
         tok_copy(off).start()
-    for c in range(1, EARLY):
-        make_hidden(c)
-        send_hidden(c)
+    send_to(EARLY, EARLY, EARLY)
     for off in range(1, M):
         spread_in(off).wait_recv()
+
     def direct(i, body):
         if not shared:
             body(cross_copy(i))
@@ -375,58 +410,33 @@
         def _():
             body(cross_copy(i))
 
-    others(lambda i: direct(i, lambda copy: copy.start()))
-    if shared:
-
-        @pl.when(g < G - 2)
-        def _():
-            extra_copy(G - 2, G - 1, 0).start()
-
-        @pl.when(g > 1)
-        def _():
-            extra_copy(1, 0, 1).start()
-
+    others(range(G - 1, 0, -1), lambda i: direct(i, lambda copy: copy.start()))
     share_out(cot_all, quarters.at[g], g, send_3, recv_3)
     cot_all[m, g] = quarters[g]
+    send_to(MID, MID, MID)
     if shared:
 
-        @pl.when(helper)
-        def _():
-            share_out(cot_x, quarters.at[edge], g, send_y, recv_y)
-            cot_x[m, g] = quarters[edge]
-
-    for c in range(EARLY, AHEAD):
-        make_hidden(c)
-        send_hidden(c)
-
-    def share_more():
-        if shared:
-
-            def more(i):
-                extra_in(i).wait_recv()
-                extra_relay(i).start()
-                share_out(cot_x, cot_x.at[m, i], i, send_y, recv_y)
-
-            extras(more)
-
+        @pl.when(g < G - 2)
+        def _():
+            extra_copy(G - 2, G - 1, 0).start()
+
+        @pl.when(g > 1)
+        def _():
+            extra_copy(1, 0, 1).start()
+
+    send_to(NEXT, NEXT, NEXT)
+
+    def share_cot(reach):
         def one(i):
             cross_in(i).wait_recv()
             share_out(cot_all, cot_all.at[m, i], i, send_3, recv_3)
 
-        others(one)
-
-    def relay_all():
-        relay(cot_all, g, send_3, recv_3)
-        others(lambda i: relay(cot_all, i, send_3, recv_3))
-        if shared:
-
-            @pl.when(helper)
-            def _():
-                relay(cot_x, g, send_y, recv_y)
-
-            extras(lambda i: relay(cot_x, i, send_y, recv_y))
-
-    def turn():
+        others(reach, one)
+
+    def relay_cot(reach):
+        others(reach, lambda i: relay(cot_all, i, send_3, recv_3))
+
+    def turn_cot():
         for i in range(G):
             share_end(cot_all, i, send_3, recv_3)
             block = jnp.concatenate([cot_all[j, i] for j in range(M)], axis=0)
@@ -438,12 +448,33 @@
                 block = jnp.concatenate([cot_all[j, g] for j in range(M)], axis=0)
                 cot_own[...] = block.T
 
-            @pl.when(helper)
-            def _():
-                for i in range(G - 1):
-                    share_end(cot_x, base + i, send_y, recv_y)
-                    block = jnp.concatenate([cot_x[j, base + i] for j in range(M)], axis=0)
-                    cot_e[:, pl.ds(i * n, n)] = block.T
+    def share_extra():
+        @pl.when(helper)
+        def _():
+            share_out(cot_x, quarters.at[edge], g, send_y, recv_y)
+            cot_x[m, g] = quarters[edge]
+
+        def more(i):
+            extra_in(i).wait_recv()
+            extra_relay(i).start()
+            share_out(cot_x, cot_x.at[m, i], i, send_y, recv_y)
+
+        extras(more)
+
+    def relay_extra():
+        @pl.when(helper)
+        def _():
+            relay(cot_x, g, send_y, recv_y)
+
+        extras(lambda i: relay(cot_x, i, send_y, recv_y))
+
+    def turn_extra():
+        @pl.when(helper)
+        def _():
+            for i in range(G - 1):
+                share_end(cot_x, base + i, send_y, recv_y)
+                block = jnp.concatenate([cot_x[j, base + i] for j in range(M)], axis=0)
+                cot_e[:, pl.ds(i * n, n)] = block.T
 
     def product(left, block):
         return jnp.dot(left, block, preferred_element_type=jnp.float32)
@@ -525,36 +556,48 @@
 
         out_ref[:, cols] = out_ref[:, cols] * inverse[0]
 
-    stage = STAGES
+    near, away = range(1, 2), range(2, G)
+    steps = [
+        (STAGES[0], lambda: relay_cot(range(1))),
+        (STAGES[1], lambda: share_cot(near)),
+        (STAGES[2], lambda: share_cot(away)),
+        (STAGES[3], lambda: relay_cot(near)),
+        (STAGES[4], lambda: relay_cot(away)),
+        (STAGES[5], turn_cot),
+    ]
+    if shared:
+        steps.insert(3, (EXTRA[0], share_extra))
+        steps.insert(6, (EXTRA[1], relay_extra))
+        steps.append((EXTRA[2], turn_extra))
     done = []
     ready = 0
     handed = 0
+    start = {}
     for t in range(chunks + 1):
         if t < chunks:
             receive(t, 1)
-        if t + AHEAD < chunks:
-            make_hidden(t + AHEAD)
-            send_hidden(t + AHEAD)
-        if t == stage[0]:
-            share_more()
-            tokens_g()
-        if t == stage[1]:
-            relay_all()
-        if t >= 1:
-            for k in range(2, G):
-                receive(t - 1, k)
-        if t == stage[2]:
-            turn()
-        late = ready
-        while t >= stage[2] and ready < t:
+        send_to(*(t + 1 + ahead for ahead in AHEAD))
+        for half in range(2):
+            if half and t >= 1:
+                for k in range(2, G):
+                    receive(t - 1, k)
+            for at, step in steps:
+                if at == 2 * t + half:
+                    step()
+            if 2 * t + half == TOKENS:
+                tokens_g()
+        turned = 2 * t + 1 >= STAGES[5]
+        turned_e = 2 * t + 1 >= EXTRA[2]
+        while turned and ready < t and (turned_e or ready not in shared):
             compute(ready)
+            start[ready] = t
             ready += 1
-        for c in range(handed, late):
-            if c in shared:
-                hand_over(c)
-            handed = c + 1
-        if t >= stage[2] + LAG:
-            for c in range(t - 1 - LAG):
+        while handed < ready and t >= start[handed] + HAND:
+            if handed in shared:
+                hand_over(handed)
+            handed += 1
+        if turned and t >= STAGES[5] // 2 + LAG:
+            for c in range(min(t - 1 - LAG, ready)):
                 if c not in done and c not in shared:
                     finish(c)
                     done.append(c)
@@ -569,7 +612,7 @@
         spread_copy(off).wait_send()
     for off in range(1, G):
         tok_copy(off).wait_send()
-    others(lambda i: direct(i, lambda copy: copy.wait_send()))
+    others(range(1, G), lambda i: direct(i, lambda copy: copy.wait_send()))
     for i in range(G):
         share_drain(cot_all, i, send_3, recv_3)
     if shared:
@@ -639,7 +682,7 @@
     bf, f32 = jnp.bfloat16, jnp.float32
     return pl.pallas_call(
         functools.partial(kernel, sizes),
-        out_shape=jax.ShapeDtypeStruct((rows, width), f32),
+        out_shape=pltpu.VMEM((rows, width), f32),
         in_specs=[smem] * 4 + [pl.BlockSpec(memory_space=pl.ANY)] * 3,
         out_specs=vmem,
         scratch_shapes=[
@@ -693,7 +736,7 @@
             dma((G,)),
         ],
         compiler_params=pltpu.CompilerParams(
-            collective_id=0, has_side_effects=True
+            collective_id=0, has_side_effects=True, vmem_limit_bytes=58_000_000
         ),
     )(
         arrival_flags,

time: 59.9 us -> 55.7 us (0.930)
  Pallas kernels: 56.2 us -> 53.7 us
  local copies, waits for them, and re-layouts: 2.85 us -> 1.23 us
    pallas_call x1, Pallas kernels: 56.2 us -> 53.7 us  [on_device(): pl.pallas_call(functools.partial(kernel, sizes), out_shape=pltpu.VMEM((ro...]
    unnamed x1, local copies, waits for them, and re-layouts: 2.85 us -> 1.23 us
where the time goes in v2:
time: 55.7 us; the launch traced here: 55.6 us
  Pallas kernels  53.7 us (96%)
  local copies, waits for them, and re-layouts  1.23 us (2%)
  between operations  0.66 us (1%)
    pallas_call x1, Pallas kernels, on_device(): pl.pallas_call(functools.partial(kernel, sizes), out_shape=pltpu.VMEM((ro...  53.7 us
    unnamed x1, local copies, waits for them, and re-layouts  1.23 us

profile of v2, /device:TPU:0, one launch (start us, length us, event | category | flops | bytes accessed | tf_op | source)
XLA Modules:
  0.0 55.6 jit_solution(11777535960690972530)
XLA Ops:
  0.7 53.7 %shard_map.73 = f32[256,1792]{1,0:T(8,128)S(1)} custom-call(s32[1]{0:T(128)S(6)} %copy.10.flags_ref, s32[1,3]{1,0:T(1,128)} %owner_ref.1, s32[1,3]{1,0:T(1,128)} %mult_ref.1, s32[8]{0:T(128)} %pieces_ref.1, bf16[192,1792]{1,0:T(8,128)(2,1)} %bitcast.3, bf16[192,1792]{1,0:T(8,128)(2,1)} %bitcast.4, bf16[192,512]{1,0:T(8,128)(2,1)} %bitcast.5), custom_call_target="tpu_custom_call" | custom-call | tf_op jit(solution)/shard_map/pallas_call | solution.py:683
  54.3 1.2 %copy.9 = f32[256,1792]{1,0:T(8,128)} copy(f32[256,1792]{1,0:T(8,128)S(1)} %shard_map.73) | data formatting | bytes 3670016

commit v3 on v2

--- a/solution.py
+++ b/solution.py
@@ -9,24 +9,32 @@
 
 TILE = 32
 CHUNK = 256
-SHARED = (2, 5)
-AHEAD = (2, 3, 4)
-EARLY = 2
-MID = 2
-NEXT = 3
-STAGES = (0, 0, 2, 2, 3, 5)
-EXTRA = (2, 7, 7)
-LAG = 1
-HAND = 2
-TOKENS = 5
+LANES = 128
+HEAD = 1
+TAIL = 3
+SHARED = (2, 6, 7)
+AHEAD = (2, 1, 7)
+EARLY = (3, 4, 2)
+MID = (2, 7, 1)
+NEXT = (3, 7, 5)
+STAGES = (4, 0, 0, 2, 4, 4)
+EXTRA = (2, 6, 7)
+LAG = 5
+HAND = 3
+TOKENS = 4
+
+
+def chunk_widths(width):
+    full, rest = divmod(width - LANES * (HEAD + TAIL), CHUNK)
+    return (LANES,) * HEAD + (CHUNK,) * full + (LANES,) * (TAIL + rest // LANES)
 
 
 def kernel(
     sizes,
-    flags_ref,
-    owner_ref,
-    mult_ref,
-    pieces_ref,
+    flags_hbm,
+    owner_hbm,
+    mult_hbm,
+    pieces_hbm,
     gate_hbm,
     lift_hbm,
     cot_hbm,
@@ -79,8 +87,16 @@
     send_f,
     recv_f,
     send_r,
+    flags_ref,
+    owner_ref,
+    mult_ref,
+    pieces_ref,
+    load_s,
 ):
-    G, R, M, slots, toks, chunks, rows, shared = sizes
+    G, R, M, slots, toks, widths, rows, shared = sizes
+    chunks = len(widths)
+    starts = [sum(widths[:c]) for c in range(chunks)]
+    wide = max(widths)
     n = slots * toks
     d = lax.axis_index("dp")
     m = lax.axis_index("mp")
@@ -210,15 +226,23 @@
             for k in range(1, G - 1):
                 body(jnp.where(is_dn, g + k, g - k))
 
+    def cut(ref, c, *index):
+        if widths[c] == wide:
+            return ref.at[index]
+        return ref.at[(*index, slice(None), pl.ds(0, widths[c]))]
+
+    def columns(c):
+        return pl.ds(starts[c], widths[c])
+
     def load(src, dst, c, sem):
         return pltpu.make_async_copy(
-            src.at[:, pl.ds(c * CHUNK, CHUNK)], dst.at[c], sem.at[c]
+            src.at[:, columns(c)], cut(dst, c, c), sem.at[c]
         )
 
     def hop(c, origin, to, sems):
         return remote(
-            hid.at[c, origin],
-            hid.at[c, origin],
+            cut(hid, c, c, origin),
+            cut(hid, c, c, origin),
             sems.at[c, origin],
             recv_h.at[c, origin],
             dev(to, r, m),
@@ -257,14 +281,18 @@
     def part_copy(c, off):
         r_to = (r + off) % R
         return remote(
-            part.at[c, r_to], arrived.at[c, r], send_p.at[c, off], recv_p.at[c, r], dev(g, r_to, m)
+            cut(part, c, c, r_to),
+            cut(arrived, c, c, r),
+            send_p.at[c, off],
+            recv_p.at[c, r],
+            dev(g, r_to, m),
         )
 
     def part_in(c, off):
         r_from = (r + off) % R
         return remote(
-            part.at[c, r_from],
-            arrived.at[c, r_from],
+            cut(part, c, c, r_from),
+            cut(arrived, c, c, r_from),
             send_p.at[c, off],
             recv_p.at[c, r_from],
             dev(g, r_from, m),
@@ -272,11 +300,21 @@
 
     def swap_e(b):
         return remote(
-            give_e.at[b], take_e.at[b], send_e.at[b], recv_e.at[b], dev(g, (r + 1) % R, m)
+            cut(give_e, shared[b], b),
+            cut(take_e, shared[b], b),
+            send_e.at[b],
+            recv_e.at[b],
+            dev(g, (r + 1) % R, m),
         )
 
     def final_e(b, to):
-        return remote(sum_e.at[b], from_e.at[b], send_f.at[b], recv_f.at[b], dev(to, r, m))
+        return remote(
+            cut(sum_e, shared[b], b),
+            cut(from_e, shared[b], b),
+            send_f.at[b],
+            recv_f.at[b],
+            dev(to, r, m),
+        )
 
     def tok_copy(off):
         return remote(
@@ -307,6 +345,19 @@
 
         lax.fori_loop(1, R, step, 0)
 
+    small = [
+        pltpu.make_async_copy(a, b, load_s.at[i])
+        for i, (a, b) in enumerate(
+            (
+                (flags_hbm, flags_ref),
+                (owner_hbm, owner_ref),
+                (mult_hbm, mult_ref),
+                (pieces_hbm, pieces_ref),
+            )
+        )
+    ]
+    for copy in small:
+        copy.start()
     load_cot = pltpu.make_async_copy(cot_hbm, cot_ref, load_c)
     load_cot.start()
     for c in range(chunks):
@@ -326,10 +377,12 @@
         greet(dev((g + off) % G, r, m))
     over_r(lambda off: greet(dev(g, (r + off) % R, m)))
 
+    for copy in small:
+        copy.wait()
     flag = flags_ref[0].astype(jnp.float32)
     scales = []
     token_sum = jnp.float32(0)
-    row = lax.broadcasted_iota(jnp.int32, (toks, CHUNK), 0)
+    row = lax.broadcasted_iota(jnp.int32, (toks, wide), 0)
     for k in range(slots):
         live = pieces_ref[owner_ref[0, k]] * TILE
         weight = flag * mult_ref[0, k].astype(jnp.float32)
@@ -342,10 +395,11 @@
         load(lift_hbm, lift_in, c, load_l).wait()
         for k in range(slots):
             rk = pl.ds(k * toks, toks)
-            v = gate_in[c, rk, :].astype(jnp.float32)
-            u = lift_in[c, rk, :].astype(jnp.float32)
-            h = v / (1.0 + jnp.exp(-v)) * u * scales[k]
-            hid[c, g, rk, :] = h.astype(jnp.bfloat16)
+            cols = pl.ds(0, widths[c])
+            v = gate_in[c, rk, cols].astype(jnp.float32)
+            u = lift_in[c, rk, cols].astype(jnp.float32)
+            h = v / (1.0 + jnp.exp(-v)) * u * scales[k][:, : widths[c]]
+            hid[c, g, rk, cols] = h.astype(jnp.bfloat16)
 
     if G >= 3:
         up_ways = (
@@ -394,7 +448,7 @@
         spread_copy(off).start()
     for off in range(1, G):
         tok_copy(off).start()
-    send_to(EARLY, EARLY, EARLY)
+    send_to(*EARLY)
     for off in range(1, M):
         spread_in(off).wait_recv()
 
@@ -413,18 +467,7 @@
     others(range(G - 1, 0, -1), lambda i: direct(i, lambda copy: copy.start()))
     share_out(cot_all, quarters.at[g], g, send_3, recv_3)
     cot_all[m, g] = quarters[g]
-    send_to(MID, MID, MID)
-    if shared:
-
-        @pl.when(g < G - 2)
-        def _():
-            extra_copy(G - 2, G - 1, 0).start()
-
-        @pl.when(g > 1)
-        def _():
-            extra_copy(1, 0, 1).start()
-
-    send_to(NEXT, NEXT, NEXT)
+    send_to(*MID)
 
     def share_cot(reach):
         def one(i):
@@ -432,6 +475,20 @@
             share_out(cot_all, cot_all.at[m, i], i, send_3, recv_3)
 
         others(reach, one)
+
+    if STAGES[1] < 0:
+        share_cot(range(1, 2))
+    if shared:
+
+        @pl.when(g < G - 2)
+        def _():
+            extra_copy(G - 2, G - 1, 0).start()
+
+        @pl.when(g > 1)
+        def _():
+            extra_copy(1, 0, 1).start()
+
+    send_to(*NEXT)
 
     def relay_cot(reach):
         others(reach, lambda i: relay(cot_all, i, send_3, recv_3))
@@ -485,32 +542,40 @@
     def main(c, left_ref, block):
         def other(off):
             r_to = (r + off) % R
-            part[c, r_to] = product(strip(left_ref, r_to), block).astype(jnp.bfloat16)
+            cut(part, c, c, r_to)[...] = product(strip(left_ref, r_to), block).astype(
+                jnp.bfloat16
+            )
             part_copy(c, off).start()
 
         over_r(other)
-        out_ref[:, pl.ds(c * CHUNK, CHUNK)] = product(strip(left_ref, r), block)
+        out_ref[:, columns(c)] = product(strip(left_ref, r), block)
+
+    def every(c):
+        return hid[c, :, :, pl.ds(0, widths[c])].reshape(G * n, widths[c])
 
     def compute(c):
         if c not in shared:
-            main(c, cot_t, hid[c].reshape(G * n, CHUNK))
+            main(c, cot_t, every(c))
             return
         b = shared.index(c)
 
         @pl.when(at_edge)
         def _():
-            main(c, cot_own, hid[c, g])
+            main(c, cot_own, hid[c, g, :, pl.ds(0, widths[c])])
 
         @pl.when(jnp.logical_not(at_edge))
         def _():
             @pl.when(helper)
             def _():
-                block = hid[c, pl.ds(base, G - 1)].reshape((G - 1) * n, CHUNK)
-                give_e[b] = product(strip(cot_e, (r + 1) % R), block).astype(jnp.bfloat16)
+                block = hid[c, pl.ds(base, G - 1), :, pl.ds(0, widths[c])]
+                block = block.reshape((G - 1) * n, widths[c])
+                cut(give_e, c, b)[...] = product(strip(cot_e, (r + 1) % R), block).astype(
+                    jnp.bfloat16
+                )
                 swap_e(b).start()
-                mine_e[b] = product(strip(cot_e, r), block)
-
-            main(c, cot_t, hid[c].reshape(G * n, CHUNK))
+                cut(mine_e, c, b)[...] = product(strip(cot_e, r), block)
+
+            main(c, cot_t, every(c))
 
     def hand_over(c):
         b = shared.index(c)
@@ -518,7 +583,8 @@
         @pl.when(helper)
         def _():
             swap_e(b).wait_recv()
-            sum_e[b] = (mine_e[b] + take_e[b].astype(jnp.float32)).astype(jnp.bfloat16)
+            total = cut(mine_e, c, b)[...] + cut(take_e, c, b)[...].astype(jnp.float32)
+            cut(sum_e, c, b)[...] = total.astype(jnp.bfloat16)
             final_e(b, edge).start()
 
     def tokens_g():
@@ -536,14 +602,16 @@
     inverse = []
 
     def finish(c):
-        cols = pl.ds(c * CHUNK, CHUNK)
+        cols = columns(c)
         if not inverse:
             total = lax.fori_loop(1, R, add_tokens, tok_sum[...])
             inverse.append((1.0 / total)[0:1, 0:1])
 
         def add_part(off):
             part_in(c, off).wait_recv()
-            out_ref[:, cols] = out_ref[:, cols] + arrived[c, (r + off) % R].astype(jnp.float32)
+            out_ref[:, cols] = out_ref[:, cols] + cut(arrived, c, c, (r + off) % R)[
+                ...
+            ].astype(jnp.float32)
 
         over_r(add_part)
         if c in shared:
@@ -552,7 +620,7 @@
             @pl.when(at_edge)
             def _():
                 final_e(b, down).wait_recv()
-                out_ref[:, cols] = out_ref[:, cols] + from_e[b].astype(jnp.float32)
+                out_ref[:, cols] = out_ref[:, cols] + cut(from_e, c, b)[...].astype(jnp.float32)
 
         out_ref[:, cols] = out_ref[:, cols] * inverse[0]
 
@@ -670,31 +738,32 @@
     _, slots, toks, width = gating_logits.shape
     feats = loss_output_grad.shape[3]
     rows = feats * M // dp
-    chunks = width // CHUNK
+    widths = chunk_widths(width)
+    chunks = len(widths)
+    wide = max(widths)
     n = slots * toks
     shared = SHARED if R == 2 and G >= 4 else ()
-    sizes = (G, R, M, slots, toks, chunks, rows, shared)
+    sizes = (G, R, M, slots, toks, widths, rows, shared)
     nb = max(len(shared), 1)
     far = G if shared else 1
-    smem = pl.BlockSpec(memory_space=pltpu.SMEM)
     vmem = pl.BlockSpec(memory_space=pltpu.VMEM)
     dma = pltpu.SemaphoreType.DMA
     bf, f32 = jnp.bfloat16, jnp.float32
     return pl.pallas_call(
         functools.partial(kernel, sizes),
         out_shape=pltpu.VMEM((rows, width), f32),
-        in_specs=[smem] * 4 + [pl.BlockSpec(memory_space=pl.ANY)] * 3,
+        in_specs=[pl.BlockSpec(memory_space=pl.ANY)] * 7,
         out_specs=vmem,
         scratch_shapes=[
-            pltpu.VMEM((chunks, n, CHUNK), bf),
-            pltpu.VMEM((chunks, n, CHUNK), bf),
+            pltpu.VMEM((chunks, n, wide), bf),
+            pltpu.VMEM((chunks, n, wide), bf),
             pltpu.VMEM((n, feats), bf),
             pltpu.VMEM((M, n // M, feats), bf),
-            pltpu.VMEM((chunks, G, n, CHUNK), bf),
+            pltpu.VMEM((chunks, G, n, wide), bf),
             pltpu.VMEM((M, G, n // M, feats), bf),
             pltpu.VMEM((feats, G * n), bf),
-            pltpu.VMEM((chunks, R, rows, CHUNK), bf),
-            pltpu.VMEM((chunks, R, rows, CHUNK), bf),
+            pltpu.VMEM((chunks, R, rows, wide), bf),
+            pltpu.VMEM((chunks, R, rows, wide), bf),
             pltpu.VMEM((8, 128), f32),
             pltpu.VMEM((G, 8, 128), f32),
             pltpu.VMEM((8, 128), f32),
@@ -702,11 +771,11 @@
             pltpu.VMEM((M, far, n // M, feats), bf),
             pltpu.VMEM((feats, n), bf),
             pltpu.VMEM((feats, (G - 1) * n), bf),
-            pltpu.VMEM((nb, rows, CHUNK), f32),
-            pltpu.VMEM((nb, rows, CHUNK), bf),
-            pltpu.VMEM((nb, rows, CHUNK), bf),
-            pltpu.VMEM((nb, rows, CHUNK), bf),
-            pltpu.VMEM((nb, rows, CHUNK), bf),
+            pltpu.VMEM((nb, rows, wide), f32),
+            pltpu.VMEM((nb, rows, wide), bf),
+            pltpu.VMEM((nb, rows, wide), bf),
+            pltpu.VMEM((nb, rows, wide), bf),
+            pltpu.VMEM((nb, rows, wide), bf),
             dma,
             dma((chunks,)),
             dma((chunks,)),
@@ -734,6 +803,11 @@
             dma((nb,)),
             dma((nb,)),
             dma((G,)),
+            pltpu.SMEM(arrival_flags.shape, jnp.int32),
+            pltpu.SMEM(block_owner_map.shape, jnp.int32),
+            pltpu.SMEM(decoder_multipliers.shape, jnp.int32),
+            pltpu.SMEM(block_piece_number.shape, jnp.int32),
+            dma((4,)),
         ],
         compiler_params=pltpu.CompilerParams(
             collective_id=0, has_side_effects=True, vmem_limit_bytes=58_000_000

time: 55.7 us -> 55 us (0.987)
  Pallas kernels: 53.7 us -> 52.9 us
    pallas_call x1, Pallas kernels: 53.7 us -> 52.9 us  [on_device(): pl.pallas_call(functools.partial(kernel, sizes), out_shape=pltpu.VMEM((ro...]
where the time goes in v3:
time: 55 us; the launch traced here: 54.8 us
  Pallas kernels  52.9 us (96%)
  local copies, waits for them, and re-layouts  1.23 us (2%)
  between operations  0.66 us (1%)
    pallas_call x1, Pallas kernels, on_device(): pl.pallas_call(functools.partial(kernel, sizes), out_shape=pltpu.VMEM((ro...  52.9 us
    unnamed x1, local copies, waits for them, and re-layouts  1.23 us

profile of v3, /device:TPU:0, one launch (start us, length us, event | category | flops | bytes accessed | tf_op | source)
XLA Modules:
  0.0 54.8 jit_solution(11155050772938438237)
XLA Ops:
  0.7 52.9 %shard_map.73 = f32[256,1792]{1,0:T(8,128)S(1)} custom-call(s32[1]{0:T(128)S(6)} %copy.10.flags_hbm, s32[1,3]{1,0:T(1,128)} %owner_hbm.1, s32[1,3]{1,0:T(1,128)} %mult_hbm.1, s32[8]{0:T(128)} %pieces_hbm.1, bf16[192,1792]{1,0:T(8,128)(2,1)} %bitcast.3, bf16[192,1792]{1,0:T(8,128)(2,1)} %bitcast.4, bf16[192,512]{1,0:T(8,128)(2,1)} %bitcast.5), custom_call_target="tpu_custom_call" | custom-call | tf_op jit(solution)/shard_map/pallas_call | solution.py:752
  53.6 1.2 %copy.9 = f32[256,1792]{1,0:T(8,128)} copy(f32[256,1792]{1,0:T(8,128)S(1)} %shard_map.73) | data formatting | bytes 3670016

commit v4 on v3

--- a/solution.py
+++ b/solution.py
@@ -10,17 +10,18 @@
 TILE = 32
 CHUNK = 256
 LANES = 128
-HEAD = 1
-TAIL = 3
-SHARED = (2, 6, 7)
-AHEAD = (2, 1, 7)
+HEAD = 2
+TAIL = 4
+SHARED = (2, 4, 6, 7, 8)
+RETURNED = (3, 5)
+AHEAD = (2, 9, 8)
 EARLY = (3, 4, 2)
-MID = (2, 7, 1)
-NEXT = (3, 7, 5)
-STAGES = (4, 0, 0, 2, 4, 4)
-EXTRA = (2, 6, 7)
+MID = (2, 6, 2)
+NEXT = (1, 2, 1)
+STAGES = (2, 0, 2, 3, 4, 4)
+EXTRA = (2, 7, 7)
 LAG = 5
-HAND = 3
+HAND = 2
 TOKENS = 4
 
 
@@ -53,7 +54,6 @@
     tok_sum,
     tok_r,
     cot_x,
-    cot_own,
     cot_e,
     mine_e,
     give_e,
@@ -87,13 +87,14 @@
     send_f,
     recv_f,
     send_r,
+    send_s,
     flags_ref,
     owner_ref,
     mult_ref,
     pieces_ref,
     load_s,
 ):
-    G, R, M, slots, toks, widths, rows, shared = sizes
+    G, R, M, slots, toks, widths, rows, shared, returned = sizes
     chunks = len(widths)
     starts = [sum(widths[:c]) for c in range(chunks)]
     wide = max(widths)
@@ -109,10 +110,9 @@
     m3 = m1 + 2 - 4 * (m1 // 2)
 
     at_edge = jnp.logical_or(g == 0, g == G - 1)
-    is_dn = g == 1
-    helper = jnp.logical_or(g == 1, g == G - 2)
-    base = jnp.where(is_dn, 1, 0)
-    edge = jnp.where(is_dn, 0, G - 1)
+    helper = jnp.logical_not(at_edge)
+    buddy = g + 1 - 2 * (g % 2)
+    paired = shared + returned
 
     def dev(g_to, r_to, m_to):
         return {"dp": g_to * R + r_to, "mp": m_to}
@@ -161,18 +161,31 @@
             dev(g_from, r, m),
         )
 
-    def extra_copy(g_to, block, s):
-        return remote(
-            quarters.at[block], cot_x.at[m, g], send_x.at[s], recv_x.at[g], dev(g_to, r, m)
-        )
-
-    def extra_relay(g_from):
+    def extra_copy(g_to):
+        return remote(
+            quarters.at[g_to + 1 - 2 * (g_to % 2)],
+            cot_x.at[m, g],
+            send_x.at[g_to],
+            recv_x.at[g],
+            dev(g_to, r, m),
+        )
+
+    def pass_cot(g_from):
         return remote(
             cot_x.at[m, g_from],
             cot_all.at[m, g_from],
             send_r.at[g_from],
             recv_2.at[g_from],
-            dev(edge, r, m),
+            dev(buddy, r, m),
+        )
+
+    def pass_extra(g_from):
+        return remote(
+            cot_all.at[m, g_from],
+            cot_x.at[m, g_from],
+            send_s.at[g_from],
+            recv_x.at[g_from],
+            dev(buddy, r, m),
         )
 
     def extra_in(g_from):
@@ -219,12 +232,6 @@
             @pl.when(g + k < G)
             def _():
                 body(g + k)
-
-    def extras(body):
-        @pl.when(helper)
-        def _():
-            for k in range(1, G - 1):
-                body(jnp.where(is_dn, g + k, g - k))
 
     def cut(ref, c, *index):
         if widths[c] == wide:
@@ -300,8 +307,8 @@
 
     def swap_e(b):
         return remote(
-            cut(give_e, shared[b], b),
-            cut(take_e, shared[b], b),
+            cut(give_e, paired[b], b),
+            cut(take_e, paired[b], b),
             send_e.at[b],
             recv_e.at[b],
             dev(g, (r + 1) % R, m),
@@ -309,8 +316,8 @@
 
     def final_e(b, to):
         return remote(
-            cut(sum_e, shared[b], b),
-            cut(from_e, shared[b], b),
+            cut(sum_e, paired[b], b),
+            cut(from_e, paired[b], b),
             send_f.at[b],
             recv_f.at[b],
             dev(to, r, m),
@@ -464,6 +471,18 @@
         def _():
             body(cross_copy(i))
 
+    def direct_x(i, body):
+        by_hand = jnp.logical_or(
+            jnp.logical_and(i == G - 1, g < G - 2), jnp.logical_and(i == 0, g > 1)
+        )
+
+        @pl.when(jnp.logical_not(by_hand))
+        def _():
+            body(extra_copy(i))
+
+    def passed(i):
+        return jnp.logical_and(helper, jnp.logical_and(i != g, i != buddy))
+
     others(range(G - 1, 0, -1), lambda i: direct(i, lambda copy: copy.start()))
     share_out(cot_all, quarters.at[g], g, send_3, recv_3)
     cot_all[m, g] = quarters[g]
@@ -472,6 +491,12 @@
     def share_cot(reach):
         def one(i):
             cross_in(i).wait_recv()
+            if shared:
+
+                @pl.when(passed(i))
+                def _():
+                    pass_extra(i).start()
+
             share_out(cot_all, cot_all.at[m, i], i, send_3, recv_3)
 
         others(reach, one)
@@ -479,15 +504,7 @@
     if STAGES[1] < 0:
         share_cot(range(1, 2))
     if shared:
-
-        @pl.when(g < G - 2)
-        def _():
-            extra_copy(G - 2, G - 1, 0).start()
-
-        @pl.when(g > 1)
-        def _():
-            extra_copy(1, 0, 1).start()
-
+        others(range(G - 1, 0, -1), lambda i: direct_x(i, lambda copy: copy.start()))
     send_to(*NEXT)
 
     def relay_cot(reach):
@@ -498,40 +515,30 @@
             share_end(cot_all, i, send_3, recv_3)
             block = jnp.concatenate([cot_all[j, i] for j in range(M)], axis=0)
             cot_t[:, pl.ds(i * n, n)] = block.T
-        if shared:
-
-            @pl.when(at_edge)
-            def _():
-                block = jnp.concatenate([cot_all[j, g] for j in range(M)], axis=0)
-                cot_own[...] = block.T
 
     def share_extra():
-        @pl.when(helper)
-        def _():
-            share_out(cot_x, quarters.at[edge], g, send_y, recv_y)
-            cot_x[m, g] = quarters[edge]
+        share_out(cot_x, quarters.at[buddy], g, send_y, recv_y)
+        cot_x[m, g] = quarters[buddy]
 
         def more(i):
             extra_in(i).wait_recv()
-            extra_relay(i).start()
+
+            @pl.when(passed(i))
+            def _():
+                pass_cot(i).start()
+
             share_out(cot_x, cot_x.at[m, i], i, send_y, recv_y)
 
-        extras(more)
+        others(range(1, G), more)
 
     def relay_extra():
-        @pl.when(helper)
-        def _():
-            relay(cot_x, g, send_y, recv_y)
-
-        extras(lambda i: relay(cot_x, i, send_y, recv_y))
+        others(range(G), lambda i: relay(cot_x, i, send_y, recv_y))
 
     def turn_extra():
-        @pl.when(helper)
-        def _():
-            for i in range(G - 1):
-                share_end(cot_x, base + i, send_y, recv_y)
-                block = jnp.concatenate([cot_x[j, base + i] for j in range(M)], axis=0)
-                cot_e[:, pl.ds(i * n, n)] = block.T
+        for i in range(G):
+            share_end(cot_x, i, send_y, recv_y)
+            block = jnp.concatenate([cot_x[j, i] for j in range(M)], axis=0)
+            cot_e[:, pl.ds(i * n, n)] = block.T
 
     def product(left, block):
         return jnp.dot(left, block, preferred_element_type=jnp.float32)
@@ -553,39 +560,34 @@
     def every(c):
         return hid[c, :, :, pl.ds(0, widths[c])].reshape(G * n, widths[c])
 
+    def doer(c):
+        return helper if c in shared else at_edge
+
     def compute(c):
-        if c not in shared:
+        if c not in paired:
             main(c, cot_t, every(c))
             return
-        b = shared.index(c)
-
-        @pl.when(at_edge)
+        b = paired.index(c)
+
+        @pl.when(doer(c))
         def _():
-            main(c, cot_own, hid[c, g, :, pl.ds(0, widths[c])])
-
-        @pl.when(jnp.logical_not(at_edge))
-        def _():
-            @pl.when(helper)
-            def _():
-                block = hid[c, pl.ds(base, G - 1), :, pl.ds(0, widths[c])]
-                block = block.reshape((G - 1) * n, widths[c])
-                cut(give_e, c, b)[...] = product(strip(cot_e, (r + 1) % R), block).astype(
-                    jnp.bfloat16
-                )
-                swap_e(b).start()
-                cut(mine_e, c, b)[...] = product(strip(cot_e, r), block)
-
-            main(c, cot_t, every(c))
+            block = every(c)
+            cut(give_e, c, b)[...] = product(strip(cot_e, (r + 1) % R), block).astype(
+                jnp.bfloat16
+            )
+            swap_e(b).start()
+            main(c, cot_t, block)
+            cut(mine_e, c, b)[...] = product(strip(cot_e, r), block)
 
     def hand_over(c):
-        b = shared.index(c)
-
-        @pl.when(helper)
+        b = paired.index(c)
+
+        @pl.when(doer(c))
         def _():
             swap_e(b).wait_recv()
             total = cut(mine_e, c, b)[...] + cut(take_e, c, b)[...].astype(jnp.float32)
             cut(sum_e, c, b)[...] = total.astype(jnp.bfloat16)
-            final_e(b, edge).start()
+            final_e(b, buddy).start()
 
     def tokens_g():
         total = tok_mine[...]
@@ -613,16 +615,21 @@
                 ...
             ].astype(jnp.float32)
 
-        over_r(add_part)
-        if c in shared:
-            b = shared.index(c)
-
-            @pl.when(at_edge)
-            def _():
-                final_e(b, down).wait_recv()
-                out_ref[:, cols] = out_ref[:, cols] + cut(from_e, c, b)[...].astype(jnp.float32)
-
-        out_ref[:, cols] = out_ref[:, cols] * inverse[0]
+        if c not in paired:
+            over_r(add_part)
+            out_ref[:, cols] = out_ref[:, cols] * inverse[0]
+            return
+
+        @pl.when(doer(c))
+        def _():
+            over_r(add_part)
+            out_ref[:, cols] = out_ref[:, cols] * inverse[0]
+
+        @pl.when(jnp.logical_not(doer(c)))
+        def _():
+            b = paired.index(c)
+            final_e(b, buddy).wait_recv()
+            out_ref[:, cols] = cut(from_e, c, b)[...].astype(jnp.float32) * inverse[0]
 
     near, away = range(1, 2), range(2, G)
     steps = [
@@ -656,21 +663,21 @@
                 tokens_g()
         turned = 2 * t + 1 >= STAGES[5]
         turned_e = 2 * t + 1 >= EXTRA[2]
-        while turned and ready < t and (turned_e or ready not in shared):
+        while turned and ready < t and (turned_e or ready not in paired):
             compute(ready)
             start[ready] = t
             ready += 1
         while handed < ready and t >= start[handed] + HAND:
-            if handed in shared:
+            if handed in paired:
                 hand_over(handed)
             handed += 1
         if turned and t >= STAGES[5] // 2 + LAG:
             for c in range(min(t - 1 - LAG, ready)):
-                if c not in done and c not in shared:
+                if c not in done and c not in paired:
                     finish(c)
                     done.append(c)
     for c in range(handed, chunks):
-        if c in shared:
+        if c in paired:
             hand_over(c)
     for c in range(chunks):
         if c not in done:
@@ -684,24 +691,21 @@
     for i in range(G):
         share_drain(cot_all, i, send_3, recv_3)
     if shared:
-
-        @pl.when(g < G - 2)
-        def _():
-            extra_copy(G - 2, G - 1, 0).wait_send()
-
-        @pl.when(g > 1)
-        def _():
-            extra_copy(1, 0, 1).wait_send()
-
-        @pl.when(helper)
-        def _():
-            for i in range(G - 1):
-                share_drain(cot_x, base + i, send_y, recv_y)
-            for k in range(1, G - 1):
-                extra_relay(jnp.where(is_dn, g + k, g - k)).wait_send()
-            for b in range(len(shared)):
+        others(range(1, G), lambda i: direct_x(i, lambda copy: copy.wait_send()))
+        for i in range(G):
+            share_drain(cot_x, i, send_y, recv_y)
+
+            @pl.when(passed(i))
+            def _():
+                pass_cot(i).wait_send()
+                pass_extra(i).wait_send()
+
+        for b, c in enumerate(paired):
+
+            @pl.when(doer(c))
+            def _():
                 swap_e(b).wait_send()
-                final_e(b, edge).wait_send()
+                final_e(b, buddy).wait_send()
 
     for c in range(chunks):
         for i in range(G):
@@ -717,7 +721,13 @@
     def drain(off):
         sum_copy(off).wait_send()
         for c in range(chunks):
-            part_copy(c, off).wait_send()
+            if c not in paired:
+                part_copy(c, off).wait_send()
+                continue
+
+            @pl.when(doer(c))
+            def _():
+                part_copy(c, off).wait_send()
 
     over_r(drain)
 
@@ -742,9 +752,10 @@
     chunks = len(widths)
     wide = max(widths)
     n = slots * toks
-    shared = SHARED if R == 2 and G >= 4 else ()
-    sizes = (G, R, M, slots, toks, widths, rows, shared)
-    nb = max(len(shared), 1)
+    shared = SHARED if R == 2 and G == 4 else ()
+    returned = RETURNED if R == 2 and G == 4 else ()
+    sizes = (G, R, M, slots, toks, widths, rows, shared, returned)
+    nb = max(len(shared) + len(returned), 1)
     far = G if shared else 1
     vmem = pl.BlockSpec(memory_space=pltpu.VMEM)
     dma = pltpu.SemaphoreType.DMA
@@ -769,8 +780,7 @@
             pltpu.VMEM((8, 128), f32),
             pltpu.VMEM((R, 8, 128), f32),
             pltpu.VMEM((M, far, n // M, feats), bf),
-            pltpu.VMEM((feats, n), bf),
-            pltpu.VMEM((feats, (G - 1) * n), bf),
+            pltpu.VMEM((feats, G * n), bf),
             pltpu.VMEM((nb, rows, wide), f32),
             pltpu.VMEM((nb, rows, wide), bf),
             pltpu.VMEM((nb, rows, wide), bf),
@@ -794,7 +804,7 @@
             dma((G,)),
             dma((R,)),
             dma((R,)),
-            dma((2,)),
+            dma((G,)),
             dma((G,)),
             dma((M, G)),
             dma((M, G)),
@@ -802,6 +812,7 @@
             dma((nb,)),
             dma((nb,)),
             dma((nb,)),
+            dma((G,)),
             dma((G,)),
             pltpu.SMEM(arrival_flags.shape, jnp.int32),
             pltpu.SMEM(block_owner_map.shape, jnp.int32),

time: 55 us -> 54.8 us (level)
  no operation moved by 1% of the time
where the time goes in v4:
time: 54.8 us; the launch traced here: 54.7 us
  Pallas kernels  52.8 us (96%)
  local copies, waits for them, and re-layouts  1.23 us (2%)
  between operations  0.66 us (1%)
    pallas_call x1, Pallas kernels, on_device(): pl.pallas_call(functools.partial(kernel, sizes), out_shape=pltpu.VMEM((ro...  52.8 us
    unnamed x1, local copies, waits for them, and re-layouts  1.23 us

profile of v4, /device:TPU:0, one launch (start us, length us, event | category | flops | bytes accessed | tf_op | source)
XLA Modules:
  0.0 54.7 jit_solution(3668089082178554232)
XLA Ops:
  0.7 52.8 %shard_map.73 = f32[256,1792]{1,0:T(8,128)S(1)} custom-call(s32[1]{0:T(128)S(6)} %copy.10.flags_hbm, s32[1,3]{1,0:T(1,128)} %owner_hbm.1, s32[1,3]{1,0:T(1,128)} %mult_hbm.1, s32[8]{0:T(128)} %pieces_hbm.1, bf16[192,1792]{1,0:T(8,128)(2,1)} %bitcast.3, bf16[192,1792]{1,0:T(8,128)(2,1)} %bitcast.4, bf16[192,512]{1,0:T(8,128)(2,1)} %bitcast.5), custom_call_target="tpu_custom_call" | custom-call | tf_op jit(solution)/shard_map/pallas_call | solution.py:763
  53.4 1.2 %copy.9 = f32[256,1792]{1,0:T(8,128)} copy(f32[256,1792]{1,0:T(8,128)S(1)} %shard_map.73) | data formatting | bytes 3670016

commit v5 on v4

--- a/solution.py
+++ b/solution.py
@@ -673,7 +673,7 @@
             handed += 1
         if turned and t >= STAGES[5] // 2 + LAG:
             for c in range(min(t - 1 - LAG, ready)):
-                if c not in done and c not in paired:
+                if c not in done and (c not in paired or t >= start[c] + HAND + 4):
                     finish(c)
                     done.append(c)
     for c in range(handed, chunks):

time: 54.8 us -> 54.8 us (level)
  no operation moved by 1% of the time
where the time goes in v5:
time: 54.8 us; the launch traced here: 54.7 us
  Pallas kernels  52.8 us (96%)
  local copies, waits for them, and re-layouts  1.23 us (2%)
  between operations  0.66 us (1%)
    pallas_call x1, Pallas kernels, on_device(): pl.pallas_call(functools.partial(kernel, sizes), out_shape=pltpu.VMEM((ro...  52.8 us
    unnamed x1, local copies, waits for them, and re-layouts  1.23 us

profile of v5, /device:TPU:0, one launch (start us, length us, event | category | flops | bytes accessed | tf_op | source)
XLA Modules:
  0.0 54.7 jit_solution(15953409080201952186)
XLA Ops:
  0.7 52.8 %shard_map.73 = f32[256,1792]{1,0:T(8,128)S(1)} custom-call(s32[1]{0:T(128)S(6)} %copy.10.flags_hbm, s32[1,3]{1,0:T(1,128)} %owner_hbm.1, s32[1,3]{1,0:T(1,128)} %mult_hbm.1, s32[8]{0:T(128)} %pieces_hbm.1, bf16[192,1792]{1,0:T(8,128)(2,1)} %bitcast.3, bf16[192,1792]{1,0:T(8,128)(2,1)} %bitcast.4, bf16[192,512]{1,0:T(8,128)(2,1)} %bitcast.5), custom_call_target="tpu_custom_call" | custom-call | tf_op jit(solution)/shard_map/pallas_call | solution.py:763
  53.4 1.2 %copy.9 = f32[256,1792]{1,0:T(8,128)} copy(f32[256,1792]{1,0:T(8,128)S(1)} %shard_map.73) | data formatting | bytes 3670016
